TPU v7x, 32 devices: a whole 2x2x4 slice. The times are simulated.
32 devices in a mesh: groups: 2 (over y), gx: 4 (over z), gy: 4 (over x, core).
Axes of the slice: x: 2, y: 2, z: 4, core: 2. Of those that a mesh axis runs over, the one named last changes fastest.
Arguments:
- tokens: bfloat16 [2, 16, 16384], P(None, 'groups', 'gx'), parts along dimension 1, may hold values from -20 to 20, as said below
- lengths: int32 [2, 16], P(None, ('groups', 'gx')), parts along dimension 1, may hold values from 1 to 1024, as said below
- norm_gain: bfloat16 [16384], P('gx'), may hold values from 0.5 to 2
- w_query: bfloat16 [16384, 8192], P('gx', 'gy'), may hold values from -1.171875 to 1.171875
- key_value_weight: bfloat16 [16384, 4, 256], P('gx', 'gy'), may hold values from -0.046875 to 0.046875
- w_out: bfloat16 [8192, 16384], P('gy', 'gx'), may hold values from -0.0625 to 0.0625
- cache: bfloat16 [2, 16, 1024, 4, 2, 128], P(None, ('groups', 'gx'), None, 'gy'), parts along dimension 1, may hold values from -16 to 16
Outputs:
- layer_out: bfloat16 [2, 16, 16384], P(None, 'groups', 'gx'), parts along dimension 1
There are 2 independent parts, one for each index of `groups`. A program takes and returns all parts, laid end to end along the dimension named above; an argument that names none is the same for every part. Nothing has to cross between parts.
Inputs may be any that keep to these rules, and one draw needn't show every extreme that they name: `tokens`: entries vary with the feature and the row. `lengths`: some rollout has exactly 1024 cached positions in every draw.
All inputs are finite; a program needn't handle non-finite values.
Results may differ from a plain program's by a relative error of at most 0.012.
The roundings to bfloat16 on the way count: a program that leaves them out, or rounds other values in their place, can miss the bound.
Values may be sent and summed in bfloat16 or wider, within the bound.
No kernel may reach another device: no remote copies, remote signals or barrier semaphores. Data moves between devices by JAX's collectives and lax.ppermute only.
A program may use at most 128 MiB of HBM per device.

v0:
```python
import jax
import jax.numpy as jnp
from jax import lax
from jax.sharding import PartitionSpec as P

MODEL_WIDTH = 16384
HEAD_SIZE = 128


def rotate(vectors, positions):
    half = vectors.shape[-1] // 2
    freq = 500000.0 ** (-2.0 * jnp.arange(half, dtype=jnp.float32) / vectors.shape[-1])
    angle = positions[..., None] * freq
    cosine = jnp.cos(angle)
    sine = jnp.sin(angle)
    first = vectors[..., :half]
    second = vectors[..., half:]
    return jnp.concatenate(
        [first * cosine - second * sine, second * cosine + first * sine], axis=-1
    )


def attend(query_sum, keyval_sum, local_squares, lengths, cache):
    batches, rows_here = lengths.shape
    score_scale = lax.rsqrt(local_squares / MODEL_WIDTH + 1e-05)
    heads_kv = keyval_sum.shape[2]
    query_group = query_sum.shape[2] // (heads_kv * HEAD_SIZE)
    query = (
        query_sum.reshape(batches, rows_here, heads_kv, query_group, HEAD_SIZE)
        * score_scale[:, :, None, None, None]
    )
    key_value = keyval_sum * score_scale[:, :, None, None]
    positions = lengths.astype(jnp.float32)
    rotated_query = rotate(query, positions[:, :, None, None]).astype(jnp.bfloat16)
    rkey = rotate(key_value[..., :HEAD_SIZE], positions[:, :, None])
    value_new = key_value[..., HEAD_SIZE:]
    inv_root = 1.0 / jnp.sqrt(jnp.float32(HEAD_SIZE))
    keys = cache[:, :, :, :, 0, :]
    values = cache[:, :, :, :, 1, :]
    scores = (
        jnp.einsum("mrkgd,mrskd->mrkgs", rotated_query, keys, preferred_element_type=jnp.float32)
        * inv_root
    )
    valid = jnp.arange(cache.shape[2], dtype=jnp.int32)[None, None, :] < lengths[:, :, None]
    scores = jnp.where(valid[:, :, None, None, :], scores, -1e30)
    new_score = (
        jnp.sum(rotated_query.astype(jnp.float32) * rkey[:, :, :, None, :], axis=-1) * inv_root
    )
    top = jnp.maximum(jnp.max(scores, axis=-1), new_score)
    weights = jnp.exp(scores - top[..., None])
    new_weight = jnp.exp(new_score - top)
    total = jnp.sum(weights, axis=-1) + new_weight
    summed = jnp.einsum(
        "mrkgs,mrskd->mrkgd",
        weights.astype(jnp.bfloat16),
        values,
        preferred_element_type=jnp.float32,
    )
    summed = summed + new_weight[..., None] * value_new[:, :, :, None, :]
    return (
        (summed / total[..., None])
        .astype(jnp.bfloat16)
        .reshape(batches, rows_here, heads_kv * query_group * HEAD_SIZE)
    )


def local(tokens, lengths, norm_gain, w_query, key_value_weight, w_out, cache):
    x_full = tokens.astype(jnp.float32)
    squares = jnp.sum(x_full * x_full, axis=-1)
    normed = (x_full * norm_gain.astype(jnp.float32)).astype(jnp.bfloat16)
    query_part = jnp.einsum("mrd,dc->mrc", normed, w_query, preferred_element_type=jnp.float32)
    keyval_part = jnp.einsum(
        "mrd,dkc->mrkc", normed, key_value_weight, preferred_element_type=jnp.float32
    )
    query_sum, keyval_sum, local_squares = (
        lax.psum_scatter(query_part, "gx", scatter_dimension=1, tiled=True),
        lax.psum_scatter(keyval_part, "gx", scatter_dimension=1, tiled=True),
        lax.psum_scatter(squares, "gx", scatter_dimension=1, tiled=True),
    )
    attended = attend(query_sum, keyval_sum, local_squares, lengths, cache)
    projected = jnp.einsum(
        "mrc,cd->mrd",
        lax.all_gather(attended, "gx", axis=1, tiled=True),
        w_out,
        preferred_element_type=jnp.float32,
    )
    summed_heads = lax.psum(projected, "gy")
    return (x_full + summed_heads).astype(jnp.bfloat16)


def solution(mesh):
    placed = (
        P(None, "groups", "gx"),
        P(None, ("groups", "gx")),
        P("gx"),
        P("gx", "gy"),
        P("gx", "gy", None),
        P("gy", "gx"),
        P(None, ("groups", "gx"), None, "gy", None, None),
    )
    return jax.shard_map(
        local, mesh=mesh, in_specs=placed, out_specs=P(None, "groups", "gx"), check_vma=False
    )
```

profile of v0, /device:TPU:0, one launch (start us, length us, event | category | flops | bytes accessed | tf_op | source)
XLA Modules:
  0.0 122.0 jit_solution(11372717634072038642)
XLA Ops:
  6.5 0.0 copy-start
  6.5 0.0 all-reduce.9.cloned.1.call-start
  6.5 0.8 convert_element_type.46
  7.4 0.0 copy-start.1
  7.4 0.0 copy-start.2
  7.4 8.8 %fusion.2 = f32[2,8,2048]{2,1,0:T(8,128)} fusion(bf16[4096,2048]{1,0:T(8,128)(2,1)} %param.10, bf16[2,8,4096]{2,1,0:T(8,128)(2,1)} %param.7, f32[4096]{0:T(1024)S(1)} %convert_element_type.46), kind=kOutput, calls=%fused_computation.2 | convolution fusion | flops 268632064 | bytes 17055744 | tf_op jit(solution)/shard_map/mrd,dc->mrc/dot_general | solution.py:71
  16.2 0.0 copy-start.3
  16.2 0.0 all-reduce.9.cloned.1.call-update
  16.2 0.0 all-reduce.7.cloned.1.call-start
  16.3 0.0 copy-done.1
  16.3 0.1 fusion.13
  16.4 0.0 copy-done.2
  16.4 0.1 iota_compare_fusion
  16.5 0.0 copy-done
  16.5 0.4 fusion.9
  16.9 0.0 copy-done.3
  16.9 0.7 dynamic-slice
  18.3 0.1 multiply_cosine_fusion.1
  18.4 20.8 %all-reduce.3 = (f32[2,8]{1,0:T(2,128)S(1)}, f32[2,8,1,256]{3,1,0,2:T(8,128)S(1)}) all-reduce(f32[2,8]{1,0:T(2,128)S(1)} %fusion.13, f32[2,8,1,256]{3,1,0,2:T(8,128)S(1)} %fusion.9), channel_id=3, replica_groups=mesh['groups'=2,'gx'=4,'gy'=4] {'gx'}, use_global_device_ids=true, to_apply=%region_2.0.clone | all-reduce | flops 4112 | bytes 32896
  39.2 0.1 fusion.32
  39.3 0.1 dynamic-slice_multiply_fusion
  39.4 0.1 fusion.29
  39.5 6.9 %fusion.35 = (bf16[2,2,1024,1,1,128]{5,4,3,2,1,0:T(2,128)(2,1)}, bf16[2,2,1024,1,1,128]{5,4,3,2,1,0:T(2,128)(2,1)}) fusion(bf16[2,2,1024,1,2,128]{5,4,3,2,1,0:T(2,128)(2,1)} %param.13), kind=kLoop, calls=%fused_computation.55 | loop fusion | bytes 4194304 | tf_op jit(solution)/shard_map/slice | solution.py:38
  46.4 0.1 maximum_bitcast_fusion
  46.5 7.3 %all-reduce.9.cloned.1.call-done = f32[2,8,2048]{2,1,0:T(8,128)} async-done(((f32[2,8,2048]{2,1,0:T(8,128)}), f32[2,8,2048]{2,1,0:T(8,128)}) %all-reduce.9.cloned.1.call-update) | async-done | bytes 131088
  53.9 0.9 constant_dynamic-slice_fusion
  54.8 0.1 broadcast_multiply_fusion
  54.9 0.1 subtract_convert_fusion
  55.0 0.2 multiply_reduce_fusion
  55.1 2.1 %fusion.36 = (f32[2,2,16]{2,1,0:T(2,128)S(1)}, f32[2,2,16,1024]{3,2,1,0:T(8,128)S(1)}) fusion(bf16[2,2,1024,1,1,128]{5,4,3,2,1,0:T(2,128)(2,1)} %get-tuple-element.9, bf16[2,2,16,64]{3,2,1,0:T(8,128)(2,1)S(1)} %bitcast.38, bf16[2,2,16,64]{3,2,1,0:T(8,128)(2,1)S(1)} %bitcast.37, pred[2,2,1024]{2,1,0:T(4,128)(4,1)S(1)} %iota_compare_fusion), kind=kOutput, calls=%fused_computation.56 | convolution fusion | flops 17006528 | bytes 1331456 | tf_op jit(solution)/shard_map/mrkgd,mrskd->mrkgs/dot_general | solution.py:41
  57.3 0.2 fusion.15
  57.5 1.9 %fusion.8 = bf16[2,2,16,128]{3,2,1,0:T(8,128)(2,1)S(1)} fusion(bf16[2,2,1024,1,1,128]{5,4,3,2,1,0:T(2,128)(2,1)} %get-tuple-element.10, f32[2,2,16,1024]{3,2,1,0:T(8,128)S(1)} %get-tuple-element.18, f32[2,2,16]{2,1,0:T(2,128)S(1)} %multiply_maximum_fusion, f32[2,2,16]{2,1,0:T(2,128)S(1)} %get-tuple-element.7, f32[2,2,128]{2,1,0:T(2,128)S(1)} %slice_bitcast_fusion, ...), kind=kOutput, calls=%fused_computation.10 | convolution fusion | flops 16941056 | bytes 1329920 | tf_op jit(solution)/shard_map/mrkgs,mrskd->mrkgd/dot_general | solution.py:53
  59.4 13.1 %all_gather.3 = bf16[2,8,2048]{2,0,1:T(2,128)(2,1)S(1)} all-gather(bf16[2,2,2048]{2,0,1:T(2,128)(2,1)S(1)} %copy.12), channel_id=1, replica_groups=mesh['groups'=2,'gx'=4,'gy'=4] {'gx'}, dimensions={1}, use_global_device_ids=true | all-gather | bytes 81920 | tf_op jit(solution)/shard_map/all_gather | solution.py:83
  72.6 8.8 %fusion = f32[2,8,4096]{2,1,0:T(8,128)} fusion(bf16[2048,4096]{1,0:T(8,128)(2,1)} %param.12, bf16[2,8,2048]{2,0,1:T(2,128)(2,1)S(1)} %all_gather.3), kind=kOutput, calls=%fused_computation | convolution fusion | flops 268435456 | bytes 17104896 | tf_op jit(solution)/shard_map/mrc,cd->mrd/dot_general | solution.py:81
  81.3 0.0 all-reduce.7.cloned.1.call-update
  81.3 32.2 %all-reduce.7.cloned.1.call-done = f32[2,8,4096]{2,1,0:T(8,128)} async-done(((f32[2,8,4096]{2,1,0:T(8,128)}), f32[2,8,4096]{2,1,0:T(8,128)}) %all-reduce.7.cloned.1.call-update) | async-done | bytes 262160 | tf_op jit(solution)/shard_map/psum | solution.py:87
  113.5 1.6 %fusion.14 = bf16[2,8,4096]{2,1,0:T(8,128)(2,1)} fusion(f32[2,8,4096]{2,1,0:T(8,128)} %all-reduce.7.cloned.1.call-done, bf16[2,8,4096]{2,1,0:T(8,128)(2,1)S(1)} %copy-done.1), kind=kLoop, calls=%fused_computation.19 | loop fusion | flops 196608 | bytes 524288 | tf_op jit(solution)/shard_map/convert_element_type | solution.py:88
  (8 shorter events, 0.1 us)
Async XLA Ops:
  6.5 10.0 %copy-start = (bf16[4096,1,256]{2,0,1:T(8,128)(2,1)S(1)}, bf16[4096,1,256]{2,0,1:T(8,128)(2,1)}, u32[]{:S(2)}) copy-start(bf16[4096,1,256]{2,0,1:T(8,128)(2,1)} %param.11) | copy-start | bytes 6291460
  6.5 47.3 %all-reduce.9.cloned.1.call-start = ((), (), s32[]{:S(2)}) async-start(), calls=%async_computation.1 | async-start | bytes 262144
  7.4 8.9 %copy-start.1 = (bf16[2,8,4096]{2,1,0:T(8,128)(2,1)S(1)}, bf16[2,8,4096]{2,1,0:T(8,128)(2,1)}, u32[]{:S(2)}) copy-start(bf16[2,8,4096]{2,1,0:T(8,128)(2,1)} %param.7) | copy-start | bytes 393220
  7.4 9.0 %copy-start.2 = (s32[2,2]{1,0:T(2,128)S(1)}, s32[2,2]{1,0:T(2,128)}, u32[]{:S(2)}) copy-start(s32[2,2]{1,0:T(2,128)} %param.8) | copy-start | bytes 52
  16.2 0.7 copy-start.3
  16.2 97.3 %all-reduce.7.cloned.1.call-start = ((), (), s32[]{:S(2)}) async-start(), calls=%async_computation | async-start | bytes 524288 | tf_op jit(solution)/shard_map/psum | solution.py:87
Sparse Core Ops, SparseCore 0:
  16.4 37.4 all-reduce.8
  81.5 31.9 all-reduce.6
where the time goes:
time: 122 us
  waiting for transfers between devices  39.5 us (32%)
  blocking collectives  33.9 us (28%)
  matrix products  22 us (18%)
  between operations  14.2 us (12%)
  local copies, waits for them, and re-layouts  8.61 us (7%)
  other arithmetic  3.71 us (3%)
    psum x1, waiting for transfers between devices, local(): summed_heads = lax.psum(projected, 'gy')  32.2 us
    unnamed x1, blocking collectives  20.8 us
    all_gather x1, blocking collectives, local(): lax.all_gather(attended, 'gx', axis=1, tiled=True)  13.1 us
    dot_general x1, matrix products, local(): jnp.einsum('mrd,dc->mrc', normed, w_query, preferred_element_type=jnp.flo...  8.81 us
    dot_general x1, matrix products, local(): jnp.einsum('mrc,cd->mrd', lax.all_gather(attended, 'gx', axis=1, tiled=Tr...  8.75 us
    unnamed x3, waiting for transfers between devices  7.38 us
    slice x1, local copies, waits for them, and re-layouts, attend(): keys = cache[:, :, :, :, 0, :]  6.95 us
  transfers between devices with their start and end apart: 2, of which 2 were waited for; matrix products, arithmetic and copies ran while one was open for 7% of the time, Pallas kernels for 0%

commit v1 on v0

--- a/solution.py
+++ b/solution.py
@@ -5,6 +5,20 @@
 
 MODEL_WIDTH = 16384
 HEAD_SIZE = 128
+
+
+def work_both_ways(value, axis, dim, make, out_dim):
+    ways, here, turn = (lax.axis_size(axis), lax.axis_index(axis), value.shape[dim])
+    earlier, later = ([], [])
+    going_up = going_down = value
+    for far in range(ways // 2 + 1):
+        earlier.append(make(going_up, (here - far) % ways * turn))
+        if 0 < far < ways - ways // 2:
+            later.append(make(going_down, (here + far) % ways * turn))
+        going_up = lax.ppermute(going_up, axis, [(d, (d + 1) % ways) for d in range(ways)])
+        going_down = lax.ppermute(going_down, axis, [(d, (d - 1) % ways) for d in range(ways)])
+    line = jnp.concatenate([*earlier[::-1], *later], axis=out_dim)
+    return jnp.roll(line, (here - ways // 2) * earlier[0].shape[out_dim], axis=out_dim)
 
 
 def rotate(vectors, positions):
@@ -78,11 +92,14 @@
         lax.psum_scatter(squares, "gx", scatter_dimension=1, tiled=True),
     )
     attended = attend(query_sum, keyval_sum, local_squares, lengths, cache)
-    projected = jnp.einsum(
-        "mrc,cd->mrd",
-        lax.all_gather(attended, "gx", axis=1, tiled=True),
-        w_out,
-        preferred_element_type=jnp.float32,
+    projected = work_both_ways(
+        attended,
+        "gx",
+        1,
+        lambda shard, at: jnp.einsum(
+            "mrc,cd->mrd", shard, w_out, preferred_element_type=jnp.float32
+        ),
+        1,
     )
     summed_heads = lax.psum(projected, "gy")
     return (x_full + summed_heads).astype(jnp.bfloat16)

time: 122 us -> 128 us (1.049)
  matrix products: 22 us -> 35.2 us
  blocking collectives: 33.9 us -> 20.8 us
  starting transfers between devices: 0.04 us -> 3.79 us
    dot_general x1 -> x4, matrix products: 8.75 us -> 22 us  [local(): jnp.einsum('mrc,cd->mrd', shard, w_out, preferred_element_type=jnp.float32)]
    all_gather x1 -> x0, blocking collectives: 13.1 us -> none  [local(): lax.all_gather(attended, 'gx', axis=1, tiled=True)]
    ppermute x0 -> x3, starting transfers between devices: none -> 3.72 us  [the longest x1 2.18 us: work_both_ways(): lax.ppermute(going_down, axis, [(d, (d - 1) % ways) for d in range(ways)])]
  transfers between devices with their start and end apart: 2 -> 5, of which waited for: 2 -> 2; matrix products, arithmetic and copies ran while one was open for 7% -> 22% of each run, Pallas kernels for 0% -> 0%
where the time goes in v1:
time: 128 us
  waiting for transfers between devices  40.4 us (32%)
  matrix products  35.2 us (28%)
  blocking collectives  20.8 us (16%)
  between operations  14.2 us (11%)
  local copies, waits for them, and re-layouts  9.63 us (8%)
  starting transfers between devices  3.79 us (3%)
  other arithmetic  3.71 us (3%)
    psum x1, waiting for transfers between devices, local(): summed_heads = lax.psum(projected, 'gy')  32.7 us
    dot_general x4, matrix products, local(): jnp.einsum('mrc,cd->mrd', shard, w_out, preferred_element_type=jnp.float32)  22 us
    unnamed x1, blocking collectives  20.8 us
    dot_general x1, matrix products, local(): jnp.einsum('mrd,dc->mrc', normed, w_query, preferred_element_type=jnp.flo...  8.78 us
    unnamed x3, waiting for transfers between devices  7.69 us
    slice x1, local copies, waits for them, and re-layouts, attend(): keys = cache[:, :, :, :, 0, :]  6.89 us
  transfers between devices with their start and end apart: 5, of which 2 were waited for; matrix products, arithmetic and copies ran while one was open for 22% of the time, Pallas kernels for 0%

profile of v1, /device:TPU:0, one launch (start us, length us, event | category | flops | bytes accessed | tf_op | source)
XLA Modules:
  0.0 127.7 jit_solution(15194413661312202251)
XLA Ops:
  6.5 0.0 copy-start
  6.5 0.0 copy-start.3
  6.5 0.0 copy-start.1
  6.5 0.0 copy-start.2
  6.5 0.0 all-reduce.9.cloned.1.call-start
  6.6 0.8 convert_element_type.46
  7.4 8.8 %fusion.8 = f32[2,8,2048]{2,1,0:T(8,128)} fusion(bf16[4096,2048]{1,0:T(8,128)(2,1)} %param.10, bf16[2,8,4096]{2,1,0:T(8,128)(2,1)} %param.7, f32[4096]{0:T(1024)S(1)} %convert_element_type.46), kind=kOutput, calls=%fused_computation.8 | convolution fusion | flops 268632064 | bytes 17055744 | tf_op jit(solution)/shard_map/mrd,dc->mrc/dot_general | solution.py:85
  16.2 0.0 all-reduce.9.cloned.1.call-update
  16.2 0.0 all-reduce.7.cloned.1.call-start
  16.3 0.0 copy-done.1
  16.3 0.1 fusion.19
  16.4 0.0 copy-done.2
  16.4 0.1 iota_compare_fusion
  16.5 0.0 copy-done
  16.5 0.4 fusion.15
  16.9 0.0 copy-done.3
  16.9 0.6 dynamic-slice
  18.1 0.1 multiply_cosine_fusion.1
  18.2 20.8 %all-reduce.3 = (f32[2,8]{1,0:T(2,128)S(1)}, f32[2,8,1,256]{3,1,0,2:T(8,128)S(1)}) all-reduce(f32[2,8]{1,0:T(2,128)S(1)} %fusion.19, f32[2,8,1,256]{3,1,0,2:T(8,128)S(1)} %fusion.15), channel_id=3, replica_groups=mesh['groups'=2,'gx'=4,'gy'=4] {'gx'}, use_global_device_ids=true, to_apply=%region_2.0.clone | all-reduce | flops 4112 | bytes 32896
  39.0 0.1 fusion.37
  39.1 0.1 dynamic-slice_multiply_fusion
  39.1 0.1 fusion.34
  39.3 6.9 %fusion.40 = (bf16[2,2,1024,1,1,128]{5,4,3,2,1,0:T(2,128)(2,1)}, bf16[2,2,1024,1,1,128]{5,4,3,2,1,0:T(2,128)(2,1)}) fusion(bf16[2,2,1024,1,2,128]{5,4,3,2,1,0:T(2,128)(2,1)} %param.13), kind=kLoop, calls=%fused_computation.61 | loop fusion | bytes 4194304 | tf_op jit(solution)/shard_map/slice | solution.py:52
  46.2 0.1 maximum_bitcast_fusion
  46.2 7.7 %all-reduce.9.cloned.1.call-done = f32[2,8,2048]{2,1,0:T(8,128)} async-done(((f32[2,8,2048]{2,1,0:T(8,128)}), f32[2,8,2048]{2,1,0:T(8,128)}) %all-reduce.9.cloned.1.call-update) | async-done | bytes 131088
  53.9 0.9 constant_dynamic-slice_fusion
  54.8 0.1 broadcast_multiply_fusion
  54.9 0.1 subtract_convert_fusion
  55.0 0.2 multiply_reduce_fusion
  55.2 2.1 %fusion.41 = (f32[2,2,16]{2,1,0:T(2,128)S(1)}, f32[2,2,16,1024]{3,2,1,0:T(8,128)S(1)}) fusion(bf16[2,2,1024,1,1,128]{5,4,3,2,1,0:T(2,128)(2,1)} %get-tuple-element.9, bf16[2,2,16,64]{3,2,1,0:T(8,128)(2,1)S(1)} %bitcast.50, bf16[2,2,16,64]{3,2,1,0:T(8,128)(2,1)S(1)} %bitcast.49, pred[2,2,1024]{2,1,0:T(4,128)(4,1)S(1)} %iota_compare_fusion), kind=kOutput, calls=%fused_computation.62 | convolution fusion | flops 17006528 | bytes 1331456 | tf_op jit(solution)/shard_map/mrkgd,mrskd->mrkgs/dot_general | solution.py:55
  57.3 0.2 fusion.21
  57.5 1.9 %fusion.14 = bf16[2,2,16,128]{3,2,1,0:T(8,128)(2,1)S(1)} fusion(bf16[2,2,1024,1,1,128]{5,4,3,2,1,0:T(2,128)(2,1)} %get-tuple-element.10, f32[2,2,16,1024]{3,2,1,0:T(8,128)S(1)} %get-tuple-element.18, f32[2,2,16]{2,1,0:T(2,128)S(1)} %multiply_maximum_fusion, f32[2,2,16]{2,1,0:T(2,128)S(1)} %get-tuple-element.7, f32[2,2,128]{2,1,0:T(2,128)S(1)} %slice_bitcast_fusion, ...), kind=kOutput, calls=%fused_computation.16 | convolution fusion | flops 16941056 | bytes 1329920 | tf_op jit(solution)/shard_map/mrkgs,mrskd->mrkgd/dot_general | solution.py:67
  59.4 0.0 slice-start
  59.5 0.0 slice-start.1
  59.5 0.0 slice-start.2
  59.5 2.2 %collective-permute-start.2 = (bf16[2,2,2048]{2,1,0:T(2,128)(2,1)S(1)}, bf16[2,2,2048]{2,1,0:T(2,128)(2,1)S(1)}, u32[]{:S(2)}, u32[]{:S(2)}) collective-permute-start(bf16[2,2,2048]{2,1,0:T(2,128)(2,1)S(1)} %reshape.199), channel_id=1, source_target_pairs={{0,12},{4,0},{8,4},{12,8},{1,13},{5,1},{9,5},{13,9},{2,14},{6,2},{... | collective-permute-start | bytes 49160 | tf_op jit(solution)/shard_map/ppermute | solution.py:19
  61.7 0.0 collective-permute-start
  61.7 8.9 %fusion.2 = f32[2,2,4096]{2,1,0:T(2,128)S(1)} fusion(bf16[2,2,2048]{2,1,0:T(2,128)(2,1)S(1)} %reshape.199, bf16[2048,4096]{1,0:T(8,128)(2,1)} %param.12), kind=kOutput, calls=%fused_computation.2 | convolution fusion | flops 67108864 | bytes 16859136 | tf_op jit(solution)/shard_map/mrc,cd->mrd/dot_general | solution.py:99
  70.6 0.0 slice-start.3
  70.6 0.0 collective-permute-done
  70.6 1.5 %collective-permute-start.1 = (bf16[2,2,2048]{2,1,0:T(2,128)(2,1)S(1)}, bf16[2,2,2048]{2,1,0:T(2,128)(2,1)S(1)}, u32[]{:S(2)}, u32[]{:S(2)}) collective-permute-start(bf16[2,2,2048]{2,1,0:T(2,128)(2,1)S(1)} %collective-permute-done), channel_id=1, source_target_pairs={{0,4},{4,8},{8,12},{12,0},{1,5},{5,9},{9,13},{13,1},{2,6},{6,10},{... | collective-permute-start | bytes 49160 | tf_op jit(solution)/shard_map/ppermute | solution.py:18
  72.2 8.2 %fusion.4 = f32[2,2,4096]{2,1,0:T(2,128)S(1)} fusion(bf16[2,2,2048]{2,1,0:T(2,128)(2,1)S(1)} %collective-permute-done, bf16[2048,4096]{1,0:T(8,128)(2,1)} %param.12), kind=kOutput, calls=%fused_computation.4 | convolution fusion | flops 67108864 | bytes 16859136 | tf_op jit(solution)/shard_map/mrc,cd->mrd/dot_general | solution.py:99
  80.3 0.0 collective-permute-done.2
  80.3 0.0 slice-done
  80.3 0.0 slice-done.1
  80.3 0.0 slice-done.2
  80.4 0.0 slice-done.3
  80.4 2.5 %fusion = f32[2,2,4096]{2,1,0:T(2,128)S(1)} fusion(bf16[2,2,2048]{2,1,0:T(2,128)(2,1)S(1)} %collective-permute-done.2, bf16[2048,4096]{1,0:T(8,128)(2,1)S(1)} %bitcast.48), kind=kOutput, calls=%fused_computation | convolution fusion | flops 67108864 | bytes 16859136 | tf_op jit(solution)/shard_map/mrc,cd->mrd/dot_general | solution.py:99
  82.8 0.0 collective-permute-done.1
  82.8 2.5 %fusion.6 = f32[2,2,4096]{2,1,0:T(2,128)S(1)} fusion(bf16[2,2,2048]{2,1,0:T(2,128)(2,1)S(1)} %collective-permute-done.1, bf16[2048,4096]{1,0:T(8,128)(2,1)S(1)} %bitcast.48), kind=kOutput, calls=%fused_computation.6 | convolution fusion | flops 67108864 | bytes 16859136 | tf_op jit(solution)/shard_map/mrc,cd->mrd/dot_general | solution.py:99
  85.3 0.4 concatenate.35
  85.7 0.7 constant_dynamic-slice_fusion.1
  86.5 0.0 all-reduce.7.cloned.1.call-update
  86.5 32.7 %all-reduce.7.cloned.1.call-done = f32[2,8,4096]{2,1,0:T(8,128)} async-done(((f32[2,8,4096]{2,1,0:T(8,128)}), f32[2,8,4096]{2,1,0:T(8,128)}) %all-reduce.7.cloned.1.call-update) | async-done | bytes 262160 | tf_op jit(solution)/shard_map/psum | solution.py:104
  119.2 1.6 %fusion.20 = bf16[2,8,4096]{2,1,0:T(8,128)(2,1)} fusion(f32[2,8,4096]{2,1,0:T(8,128)} %all-reduce.7.cloned.1.call-done, bf16[2,8,4096]{2,1,0:T(8,128)(2,1)S(1)} %copy-done.1), kind=kLoop, calls=%fused_computation.25 | loop fusion | flops 196608 | bytes 524288 | tf_op jit(solution)/shard_map/convert_element_type | solution.py:105
  (8 shorter events, 0.1 us)
Async XLA Ops:
  6.5 10.0 %copy-start = (bf16[4096,1,256]{2,0,1:T(8,128)(2,1)S(1)}, bf16[4096,1,256]{2,0,1:T(8,128)(2,1)}, u32[]{:S(2)}) copy-start(bf16[4096,1,256]{2,0,1:T(8,128)(2,1)} %param.11) | copy-start | bytes 6291460
  6.5 10.4 %copy-start.3 = (u32[32]{0:T(128)S(1)}, u32[32]{0:T(128)}, u32[]{:S(2)}) copy-start(u32[32]{0:T(128)} %constant.58) | copy-start | bytes 388
  6.5 9.8 %copy-start.1 = (bf16[2,8,4096]{2,1,0:T(8,128)(2,1)S(1)}, bf16[2,8,4096]{2,1,0:T(8,128)(2,1)}, u32[]{:S(2)}) copy-start(bf16[2,8,4096]{2,1,0:T(8,128)(2,1)} %param.7) | copy-start | bytes 393220
  6.5 9.9 %copy-start.2 = (s32[2,2]{1,0:T(2,128)S(1)}, s32[2,2]{1,0:T(2,128)}, u32[]{:S(2)}) copy-start(s32[2,2]{1,0:T(2,128)} %param.8) | copy-start | bytes 52
  6.5 47.3 %all-reduce.9.cloned.1.call-start = ((), (), s32[]{:S(2)}) async-start(), calls=%async_computation.1 | async-start | bytes 262144
  16.2 103.0 %all-reduce.7.cloned.1.call-start = ((), (), s32[]{:S(2)}) async-start(), calls=%async_computation | async-start | bytes 524288 | tf_op jit(solution)/shard_map/psum | solution.py:104
  59.4 20.9 %slice-start = ((s8[16777216]{0:T(1024)(128)(4,1)}), s8[4194304]{0:T(1024)(128)(4,1)S(1)}, s32[]{:S(2)}) async-start(s8[16777216]{0:T(1024)(128)(4,1)} %bitcast.47), calls=%async_computation.2 | async-start | bytes 8388608
  59.5 20.9 %slice-start.1 = ((s8[16777216]{0:T(1024)(128)(4,1)}), s8[4194304]{0:T(1024)(128)(4,1)S(1)}, s32[]{:S(2)}) async-start(s8[16777216]{0:T(1024)(128)(4,1)} %bitcast.47), calls=%async_computation.3 | async-start | bytes 8388608
  59.5 20.9 %slice-start.2 = ((s8[16777216]{0:T(1024)(128)(4,1)}), s8[4194304]{0:T(1024)(128)(4,1)S(1)}, s32[]{:S(2)}) async-start(s8[16777216]{0:T(1024)(128)(4,1)} %bitcast.47), calls=%async_computation.4 | async-start | bytes 8388608
  59.5 20.8 %collective-permute-start.2 = (bf16[2,2,2048]{2,1,0:T(2,128)(2,1)S(1)}, bf16[2,2,2048]{2,1,0:T(2,128)(2,1)S(1)}, u32[]{:S(2)}, u32[]{:S(2)}) collective-permute-start(bf16[2,2,2048]{2,1,0:T(2,128)(2,1)S(1)} %reshape.199), channel_id=1, source_target_pairs={{0,12},{4,0},{8,4},{12,8},{1,13},{5,1},{9,5},{13,9},{2,14},{6,2},{... | collective-permute-start | bytes 49160 | tf_op jit(solution)/shard_map/ppermute | solution.py:19
  61.7 9.0 %collective-permute-start = (bf16[2,2,2048]{2,1,0:T(2,128)(2,1)S(1)}, bf16[2,2,2048]{2,1,0:T(2,128)(2,1)S(1)}, u32[]{:S(2)}, u32[]{:S(2)}) collective-permute-start(bf16[2,2,2048]{2,1,0:T(2,128)(2,1)S(1)} %reshape.199), channel_id=1, source_target_pairs={{0,4},{4,8},{8,12},{12,0},{1,5},{5,9},{9,13},{13,1},{2,6},{6,10},{... | collective-permute-start | bytes 49160 | tf_op jit(solution)/shard_map/ppermute | solution.py:18
  70.6 9.8 %slice-start.3 = ((s8[16777216]{0:T(1024)(128)(4,1)}), s8[4194304]{0:T(1024)(128)(4,1)S(1)}, s32[]{:S(2)}) async-start(s8[16777216]{0:T(1024)(128)(4,1)} %bitcast.47), calls=%async_computation.5 | async-start | bytes 8388608
  70.6 12.2 %collective-permute-start.1 = (bf16[2,2,2048]{2,1,0:T(2,128)(2,1)S(1)}, bf16[2,2,2048]{2,1,0:T(2,128)(2,1)S(1)}, u32[]{:S(2)}, u32[]{:S(2)}) collective-permute-start(bf16[2,2,2048]{2,1,0:T(2,128)(2,1)S(1)} %collective-permute-done), channel_id=1, source_target_pairs={{0,4},{4,8},{8,12},{12,0},{1,5},{5,9},{9,13},{13,1},{2,6},{6,10},{... | collective-permute-start | bytes 49160 | tf_op jit(solution)/shard_map/ppermute | solution.py:18
Sparse Core Ops, SparseCore 0:
  16.4 37.4 all-reduce.8
  86.6 32.5 all-reduce.6
